TPU v7x, 32 devices: a 4x2x2 block of a 4x4x8 slice. The times are simulated.
32 devices in a mesh: dp: 4 (over y, z), tp: 8 (over x, core).
Axes of the slice: x: 4, y: 2, z: 2, core: 2. Of those that a mesh axis runs over, the one named last changes fastest.
The devices are a block of a 4x4x8 slice.
Arguments:
- hidden: bfloat16 [8, 64, 2048], P('dp', None, 'tp'), parts along dimension 0
- ln_scale: float32 [2048], P('tp')
- w_head: bfloat16 [2048, 256384], P(None, 'tp')
- targets: int32 [8, 64], P('dp'), parts along dimension 0
- valid_mask: int32 [8, 64], P('dp'), parts along dimension 0
Outputs:
- output 1: float32 [8, 64], P('dp'), parts along dimension 0
- output 2: float32 [8], P('dp'), parts along dimension 0
There are 4 independent parts. A program takes and returns all parts, laid end to end along the dimension named above; an argument that names none is the same for every part.
All inputs are finite; a program needn't handle non-finite values.
Results may differ from a plain program's by a relative error of at most 0.001.
Values are sent between devices in bfloat16 or wider.
A program may use at most 768 MiB of HBM per device.

v0:
```python
import functools

import jax
import jax.numpy as jnp
from jax import lax
from jax.experimental import pallas as pl
from jax.experimental.pallas import tpu as pltpu
from jax.sharding import PartitionSpec as P

NORM_EPS = 1e-6
TILE = 1024
LANES = 128
CHUNK = 128
STRIP = 32
SLOTS = 13
UNROLL = 4
PAIR = True
MESH = pl.DeviceIdType.MESH
NEG_INF = float("-inf")


def plan(v_local, pair):
    sides = 2 if pair else 1
    half = -(-v_local // (16 * sides)) * 16
    return half, half // TILE, half % TILE


def kernel(cfg, h_hbm, g_hbm, w_hbm, tgt_hbm, out_ref,
           hb, gb, tg, xb, qb, wb, wt, za, zb, st, sbuf,
           loc_sem, w_sem, t_sem, snd, rcv, g_snd, g_rcv, f_snd, f_rcv):
    tp, pair, v_local = cfg
    groups = 2 if pair else 1
    rows, feat = h_hbm.shape
    seqs, slen = tgt_hbm.shape
    half, n_full, tail = plan(v_local, pair)
    nx = tp // 2
    me_dp = lax.axis_index("dp")
    me = lax.axis_index("tp")
    x, core = me // 2, me % 2
    side = me_dp % 2 if pair else 0
    mate_dp = me_dp + 1 - 2 * (me_dp % 2) if pair else me_dp
    right = 2 * ((x + 1) % nx) + core
    left = 2 * ((x + nx - 1) % nx) + core
    far = 2 * ((x + 2) % nx) + core
    flip = 1 - 2 * core
    other = me + flip
    row0 = side * (v_local - half)

    h_cp = pltpu.make_async_copy(h_hbm, hb.at[0, me], loc_sem.at[0])
    g_cp = pltpu.make_async_copy(g_hbm, gb.at[me], loc_sem.at[1])
    t_in = pltpu.make_async_copy(tgt_hbm, tg.at[0], loc_sem.at[2])
    for cp in (h_cp, g_cp, t_in):
        cp.start()

    def w_copy(i):
        slot = i % SLOTS if isinstance(i, int) else lax.rem(i, SLOTS)
        start = row0 + i * TILE
        return pltpu.make_async_copy(
            w_hbm.at[pl.ds(pl.multiple_of(start, 16), TILE), :], wb.at[slot], w_sem.at[slot])

    tail_cp = pltpu.make_async_copy(
        w_hbm.at[pl.ds(pl.multiple_of(row0 + n_full * TILE, 16), tail), :], wt, t_sem.at[0])
    def fetch(first, stop):
        for i in range(first, min(stop, n_full)):
            w_copy(i).start()

    fetch(0, 1)

    to_right, to_left, to_other, to_mate = (me_dp, right), (me_dp, left), (me_dp, other), (mate_dp, me)
    near = [to_right, to_left, to_other]
    mate_right, mate_left = (mate_dp, right), (mate_dp, left)
    if pair:
        near += [to_mate, mate_right, mate_left]
    barrier = pltpu.get_barrier_semaphore()
    for dev in near:
        pl.semaphore_signal(barrier, inc=1, device_id=dev, device_id_type=MESH)
    h_cp.wait()
    g_cp.wait()
    t_in.wait()
    pl.semaphore_wait(barrier, len(near))

    started = []

    def remote(src, dst, s_sem, r_sem, dev):
        return pltpu.make_async_remote_copy(
            src_ref=src, dst_ref=dst, send_sem=s_sem, recv_sem=r_sem, device_id=dev, device_id_type=MESH)

    def send(grp, origin, part, flow, dev, grp_dst):
        cp = remote(hb.at[grp, origin, part], hb.at[grp_dst, origin, part], snd.at[flow], rcv.at[flow], dev)
        cp.start()
        started.append(cp)

    def arrived(grp, origin, part, flow):
        ref = hb.at[grp, origin, part]
        remote(ref, ref, snd.at[flow], rcv.at[flow], to_other).wait_recv()

    def g_send(origin, flow, dev):
        cp = remote(gb.at[origin], gb.at[origin], g_snd.at[flow], g_rcv.at[flow], dev)
        cp.start()
        started.append(cp)

    def g_arrived(origin, flow):
        remote(gb.at[origin], gb.at[origin], g_snd.at[flow], g_rcv.at[flow], to_other).wait_recv()

    RING, SIDE, MATE, MSIDE = 0, 8, 16, 24
    lo, hi, both = pl.ds(0, rows // 2), pl.ds(rows // 2, rows // 2), pl.ds(0, rows)
    lane = [me, left, right, far]

    def both_groups(part, flow, own_dev, mate_dev):
        send(0, me, part, RING + flow, own_dev, 0)
        if pair:
            send(0, me, part, MATE + flow, mate_dev, 1)

    both_groups(lo, 0, to_right, mate_right)
    both_groups(hi, 1, to_left, mate_left)
    both_groups(hi, 2, to_right, mate_right)
    both_groups(lo, 3, to_left, mate_left)
    if pair:
        send(0, me, both, MATE + 6, to_mate, 1)
    send(0, me, both, SIDE + 0, to_other, 0)
    g_send(me, 0, to_right)
    g_send(me, 1, to_left)
    g_send(me, 3, to_other)
    if pair:
        t_cp = remote(tg.at[0], tg.at[1], g_snd.at[7], g_rcv.at[7], to_mate)
        t_cp.start()
        started.append(t_cp)
    fetch(1, 3)
    flows = ((0, RING, SIDE), (1, MATE, MSIDE))[:groups]
    for grp, ring, _ in flows:
        arrived(grp, left, lo, ring + 0)
        send(grp, left, lo, ring + 4, to_right, grp)
        arrived(grp, right, hi, ring + 1)
        send(grp, right, hi, ring + 5, to_left, grp)
    fetch(3, 5)
    g_arrived(left, 0)
    g_send(left, 2, to_right)
    g_send(left, 4, to_other)
    g_arrived(right, 1)
    g_send(right, 5, to_other)
    if pair:
        arrived(1, me, both, MATE + 6)
        send(1, me, both, MSIDE + 0, to_other, 1)
    for grp, ring, across in flows:
        arrived(grp, left, hi, ring + 2)
        send(grp, left, both, across + 1, to_other, grp)
        arrived(grp, right, lo, ring + 3)
        send(grp, right, both, across + 2, to_other, grp)
    fetch(5, 7)
    g_arrived(far, 2)
    g_send(far, 6, to_other)
    for grp, ring, across in flows:
        arrived(grp, far, lo, ring + 4)
        arrived(grp, far, hi, ring + 5)
        send(grp, far, both, across + 3, to_other, grp)
    fetch(7, SLOTS)
    for k in range(4):
        arrived(0, lane[k] + flip, both, SIDE + k)
    for k, origin in ((3, me), (4, left), (5, right), (6, far)):
        g_arrived(origin + flip, k)

    def squares(grp, blocks, fresh_sum):
        for r in range(0, rows, STRIP):
            acc = jnp.zeros((STRIP, LANES), jnp.float32) if fresh_sum else qb[r:r + STRIP, :]
            for j in blocks:
                v = hb[grp, j, r:r + STRIP, :].astype(jnp.float32)
                sq = v * v
                for c in range(0, feat, LANES):
                    acc += sq[:, c:c + LANES]
            qb[r:r + STRIP, :] = acc

    def normalize(grp):
        for r in range(0, rows, STRIP):
            total = jnp.sum(qb[r:r + STRIP, :], axis=1, keepdims=True)
            inv = lax.rsqrt(total / (feat * tp) + NORM_EPS)
            for j in range(tp):
                v = hb[grp, j, r:r + STRIP, :].astype(jnp.float32)
                xb[grp * rows + r:grp * rows + r + STRIP, j * feat:(j + 1) * feat] = (
                    v * inv * gb[j]).astype(jnp.bfloat16)

    def places_of(grp):
        ids = jnp.concatenate([tg[grp, b:b + 1, :] for b in range(seqs)], axis=1)
        return jnp.broadcast_to(ids - me * v_local, (8, rows)) - lax.broadcasted_iota(jnp.int32, (8, rows), 0)

    def fresh():
        return (jnp.full((8, rows), NEG_INF, jnp.float32), jnp.zeros((8, rows), jnp.float32),
                jnp.zeros((8, rows), jnp.float32))

    def dot(z_ref, w_rows, n, cols=groups * rows):
        cut = -(-n // 32) * 16
        for r0, r1 in ((0, cut), (cut, n)):
            z_ref[r0:r1, 0:cols] = lax.dot_general(
                w_rows(r0, r1), xb[0:cols, :], (((1,), (1,)), ((), ())), preferred_element_type=jnp.float32)

    def tile_rows(slot):
        return lambda r0, r1: wb[slot, r0:r1, :]

    def absorb(z_ref, base, n, state, places, first_masked=None):
        m, s, t = state
        for r in range(0, n, CHUNK):
            zs, hits = [], []
            for q in range(r, min(r + CHUNK, n), 8):
                z = z_ref[q:q + 8, 0:m.shape[1]]
                hit = places == base + q
                if first_masked is not None and q >= first_masked:
                    z = jnp.where(side > 0, z, NEG_INF)
                    hit = hit & (side > 0)
                zs.append(z)
                hits.append(hit)
            tree = list(zs)
            while len(tree) > 1:
                tree = [jnp.maximum(*tree[i:i + 2]) if i + 1 < len(tree) else tree[i]
                        for i in range(0, len(tree), 2)]
            top = jnp.maximum(m, tree[0])
            es = [jnp.exp(z - top) for z in zs]
            while len(es) > 1:
                es = [es[i] + es[i + 1] if i + 1 < len(es) else es[i] for i in range(0, len(es), 2)]
            s = s * jnp.exp(m - top) + es[0]
            for z, hit in zip(zs, hits):
                t = jnp.where(hit, z, t)
            m = top
        return m, s, t

    squares(0, range(tp), True)
    normalize(0)
    own_places, state = places_of(0), fresh()
    if pair:
        for k in range(3):
            arrived(1, lane[k] + flip, both, MSIDE + k)
        squares(1, [j for k in range(3) for j in (lane[k], lane[k] + flip)], True)
        arrived(1, far + flip, both, MSIDE + 3)
        squares(1, (far, far + flip), False)
        t_cp.wait_recv()
        normalize(1)
        places = jnp.concatenate([own_places, places_of(1)], axis=1)
        state = tuple(jnp.concatenate(p, axis=1) for p in zip(state, fresh()))
    else:
        places = own_places

    bufs = (za, zb)

    def refill(i):
        if 0 <= i - 1 < n_full - SLOTS:
            w_copy(i - 1 + SLOTS).start()
            if i + SLOTS == n_full:
                tail_cp.start()

    def run(first, count, state):
        for q in range(count):
            i = first + q
            nxt = (i + 1) % SLOTS if isinstance(i, int) else lax.rem(i + 1, SLOTS)
            dot(bufs[(q + 1) % 2], tile_rows(nxt), TILE)
            state = absorb(bufs[q % 2], row0 + i * TILE, TILE, state, places)
        return state

    trips, rest = divmod(n_full - 1, UNROLL)
    if rest % 2 or UNROLL % 2 or n_full != SLOTS + rest:
        raise ValueError("tile count")
    for i in range(rest + 1):
        w_copy(i).wait()
    dot(za, tile_rows(0), TILE)
    state = run(0, rest, state)
    for i in range(1, rest + 1):
        refill(i)

    def trip(j, state):
        first = rest + UNROLL * j
        for q in range(UNROLL):
            w_copy(first + q + 1).wait()
        return run(first, UNROLL, state)

    state = lax.fori_loop(0, trips, trip, state)
    tail_cp.wait()
    dot(bufs[1], lambda r0, r1: wt[r0:r1, :], tail)
    state = absorb(bufs[0], row0 + (n_full - 1) * TILE, TILE, state, places)
    twice = groups * half - v_local
    m, s, t = absorb(bufs[1], row0 + n_full * TILE, tail, state, places, tail - twice if twice else None)

    top = jnp.max(m, axis=0, keepdims=True)
    total = jnp.sum(s * jnp.exp(m - top), axis=0, keepdims=True)
    picked = jnp.sum(t, axis=0, keepdims=True)
    for grp in range(groups):
        gs = slice(grp * rows, (grp + 1) * rows)
        st[grp] = jnp.concatenate(
            [top[:, gs], total[:, gs], picked[:, gs], jnp.zeros((5, rows), jnp.float32)], axis=0)

    if pair:
        for k in range(tp):
            cp = remote(st.at[1], sbuf.at[1, me], f_snd.at[tp + k], f_rcv.at[tp + k], (mate_dp, (me + k) % tp))
            cp.start()
            started.append(cp)
    for k in range(1, tp):
        cp = remote(st.at[0], sbuf.at[0, me], f_snd.at[k], f_rcv.at[k], (me_dp, (me + k) % tp))
        cp.start()
        started.append(cp)
    sbuf[0, me] = st[0]
    for k in range(1, tp):
        ref = sbuf.at[0, (me + tp - k) % tp]
        remote(ref, ref, f_snd.at[k], f_rcv.at[k], to_other).wait_recv()
    if pair:
        for k in range(tp):
            ref = sbuf.at[1, (me + tp - k) % tp]
            remote(ref, ref, f_snd.at[tp + k], f_rcv.at[tp + k], to_other).wait_recv()

    parts = [sbuf[g, j] for g in range(groups) for j in range(tp)]
    top = functools.reduce(jnp.maximum, parts)[0:1, :]
    total = functools.reduce(jnp.add, [p[1:2, :] * jnp.exp(p[0:1, :] - top) for p in parts])
    picked = functools.reduce(jnp.add, parts)[2:3, :]
    logp = picked - (top + jnp.log(total))
    for b in range(seqs):
        out_ref[b:b + 1, :] = logp[:, b * slen:(b + 1) * slen]
    for cp in started:
        cp.wait_send()


def solution(mesh):
    tp = mesh.shape["tp"]
    pair = PAIR and mesh.shape["dp"] % 2 == 0

    def local_score(hidden, ln_scale, w_head, targets, valid_mask):
        seqs, slen, feat = hidden.shape
        rows, d, v_local = seqs * slen, w_head.shape[0], w_head.shape[1]
        groups = 2 if pair else 1
        tail = plan(v_local, pair)[2]
        f32, bf16 = jnp.float32, jnp.bfloat16
        dma = pltpu.SemaphoreType.DMA
        logp = pl.pallas_call(
            functools.partial(kernel, (tp, pair, v_local)),
            out_shape=jax.ShapeDtypeStruct((seqs, slen), f32),
            in_specs=[pl.BlockSpec(memory_space=pl.ANY)] * 4,
            out_specs=pl.BlockSpec(memory_space=pltpu.VMEM),
            scratch_shapes=[
                pltpu.VMEM((groups, tp, rows, feat), bf16),
                pltpu.VMEM((tp, 1, feat), f32),
                pltpu.VMEM((2, seqs, slen), jnp.int32),
                pltpu.VMEM((groups * rows, d), bf16),
                pltpu.VMEM((rows, LANES), f32),
                pltpu.VMEM((SLOTS, TILE, d), bf16),
                pltpu.VMEM((tail, d), bf16),
                pltpu.VMEM((TILE, groups * rows), f32),
                pltpu.VMEM((TILE, groups * rows), f32),
                pltpu.VMEM((groups, 8, rows), f32),
                pltpu.VMEM((groups, tp, 8, rows), f32),
                dma((3,)), dma((SLOTS,)), dma((1,)),
                dma((32,)), dma((32,)), dma((8,)), dma((8,)), dma((2 * tp,)), dma((2 * tp,)),
            ],
            compiler_params=pltpu.CompilerParams(
                collective_id=0, has_side_effects=True, vmem_limit_bytes=67043328),
            name="score",
        )(hidden.reshape(rows, feat), ln_scale.reshape(1, feat), w_head.T, targets)
        token_logp = valid_mask.astype(f32) * logp
        return token_logp, jnp.sum(token_logp, axis=1)

    return jax.shard_map(
        local_score,
        mesh=mesh,
        in_specs=(P("dp", None, "tp"), P("tp"), P(None, "tp"), P("dp", None), P("dp", None)),
        out_specs=(P("dp", None), P("dp")),
        check_vma=False,
    )
```

profile of v0, /device:TPU:81, one launch (start us, length us, event | category | flops | bytes accessed | tf_op | source)
XLA Modules:
  0.0 44.0 jit_solution(8940461577006911491)
XLA Ops:
  0.6 41.5 %score.1 = f32[2,64]{1,0:T(2,128)} custom-call(bf16[128,256]{1,0:T(8,128)(2,1)} %bitcast.3, f32[1,256]{1,0:T(1,128)} %bitcast.4, bf16[32048,2048]{1,0:T(8,128)(2,1)} %bitcast.2.w_hbm, s32[2,64]{1,0:T(2,128)} %tgt_hbm.1), custom_call_target="tpu_custom_call" | custom-call | tf_op jit(solution)/shard_map/score/pallas_call | solution.py:327
  42.1 1.9 %fusion = (f32[2]{0:T(128)}, f32[2,64]{1,0:T(2,128)}) fusion(f32[2,64]{1,0:T(2,128)} %score.1, s32[2,64]{1,0:T(2,128)} %param.9), kind=kLoop, calls=%fused_computation.1 | loop fusion | flops 382 | bytes 1544 | tf_op jit(solution)/shard_map/reduce_sum | solution.py:352
where the time goes:
time: 44.1 us; the launch traced here: 44 us
  Pallas kernels  41.5 us (94%)
  other arithmetic  1.87 us (4%)
  between operations  0.64 us (1%)
    pallas_call x1, Pallas kernels, local_score(): pl.pallas_call(functools.partial(kernel, (tp, pair, v_local)), out_shape=...  41.5 us
    reduce_sum x1, other arithmetic, local_score(): return (token_logp, jnp.sum(token_logp, axis=1))  1.87 us

commit v1 on v0

--- a/solution.py
+++ b/solution.py
@@ -49,8 +49,7 @@
     h_cp = pltpu.make_async_copy(h_hbm, hb.at[0, me], loc_sem.at[0])
     g_cp = pltpu.make_async_copy(g_hbm, gb.at[me], loc_sem.at[1])
     t_in = pltpu.make_async_copy(tgt_hbm, tg.at[0], loc_sem.at[2])
-    for cp in (h_cp, g_cp, t_in):
-        cp.start()
+    h_cp.start()
 
     def w_copy(i):
         slot = i % SLOTS if isinstance(i, int) else lax.rem(i, SLOTS)
@@ -64,8 +63,6 @@
         for i in range(first, min(stop, n_full)):
             w_copy(i).start()
 
-    fetch(0, 1)
-
     to_right, to_left, to_other, to_mate = (me_dp, right), (me_dp, left), (me_dp, other), (mate_dp, me)
     near = [to_right, to_left, to_other]
     mate_right, mate_left = (mate_dp, right), (mate_dp, left)
@@ -74,6 +71,10 @@
     barrier = pltpu.get_barrier_semaphore()
     for dev in near:
         pl.semaphore_signal(barrier, inc=1, device_id=dev, device_id_type=MESH)
+    g_cp.start()
+    t_in.start()
+
+    fetch(0, 1)
     h_cp.wait()
     g_cp.wait()
     t_in.wait()
@@ -294,6 +295,8 @@
         cp.start()
         started.append(cp)
     sbuf[0, me] = st[0]
+    for cp in started:
+        cp.wait_send()
     for k in range(1, tp):
         ref = sbuf.at[0, (me + tp - k) % tp]
         remote(ref, ref, f_snd.at[k], f_rcv.at[k], to_other).wait_recv()
@@ -309,8 +312,6 @@
     logp = picked - (top + jnp.log(total))
     for b in range(seqs):
         out_ref[b:b + 1, :] = logp[:, b * slen:(b + 1) * slen]
-    for cp in started:
-        cp.wait_send()
 
 
 def solution(mesh):

time: 44.1 us -> 44 us (level)
  no operation moved by 1% of the time
where the time goes in v1:
time: 44 us; the launch traced here: 43.9 us
  Pallas kernels  41.4 us (94%)
  other arithmetic  1.87 us (4%)
  between operations  0.64 us (1%)
    pallas_call x1, Pallas kernels, local_score(): pl.pallas_call(functools.partial(kernel, (tp, pair, v_local)), out_shape=...  41.4 us
    reduce_sum x1, other arithmetic, local_score(): return (token_logp, jnp.sum(token_logp, axis=1))  1.87 us

profile of v1, /device:TPU:81, one launch (start us, length us, event | category | flops | bytes accessed | tf_op | source)
XLA Modules:
  0.0 43.9 jit_solution(8773682157470350287)
XLA Ops:
  0.6 41.4 %score.1 = f32[2,64]{1,0:T(2,128)} custom-call(bf16[128,256]{1,0:T(8,128)(2,1)} %bitcast.3, f32[1,256]{1,0:T(1,128)} %bitcast.4, bf16[32048,2048]{1,0:T(8,128)(2,1)} %bitcast.2.w_hbm, s32[2,64]{1,0:T(2,128)} %tgt_hbm.1), custom_call_target="tpu_custom_call" | custom-call | tf_op jit(solution)/shard_map/score/pallas_call | solution.py:328
  42.1 1.9 %fusion = (f32[2]{0:T(128)}, f32[2,64]{1,0:T(2,128)}) fusion(f32[2,64]{1,0:T(2,128)} %score.1, s32[2,64]{1,0:T(2,128)} %param.9), kind=kLoop, calls=%fused_computation.1 | loop fusion | flops 382 | bytes 1544 | tf_op jit(solution)/shard_map/reduce_sum | solution.py:353
